TPU v7x, 32 devices: a whole 2x2x4 slice. The times are simulated.
32 devices in a mesh: lat: 4 (over z), lon: 8 (over y, x, core).
Axes of the slice: x: 2, y: 2, z: 4, core: 2. Of those that a mesh axis runs over, the one named last changes fastest.
Arguments:
- observations: bfloat16 [49152, 128], P(('lat', 'lon')), may hold values from -6 to 6
- owner_device: int32 [49152, 1], P(('lat', 'lon')), may hold values from 0 to 31; in each aligned block of 1536 rows (0 to 1535, 1536 to 3071, ...) at most 96 rows name the same one
- local_cell: int32 [49152], P(('lat', 'lon')), may hold values from 0 to 383
- valid_counts: int32 [32], P(('lat', 'lon')), may hold values from 768 to 1536
- weight_in: bfloat16 [128, 256], replicated, may hold values from -0.5 to 0.5
- bias_in: float32 [256], replicated, may hold values from -3 to 3
- weight_out: bfloat16 [256, 256], replicated, may hold values from -0.375 to 0.375
- kernel_taps: float32 [9, 256], replicated, may hold values from -2 to 2
- cotangent: bfloat16 [64, 192, 256], P(('lat', 'lon')), may hold values from -6 to 6
Outputs:
- grid_out: bfloat16 [64, 192, 256], P(('lat', 'lon'))
- grad_weight_in: float32 [128, 256], replicated
- grad_bias_in: float32 [256], replicated
- grad_weight_out: float32 [256, 256], replicated
- grad_kernel: float32 [9, 256], replicated
Inputs may be any that keep to these rules, and one draw needn't show every extreme that they name: `owner_device`: within the rows of one block, at most 96 rows name one owner, and in every draw some block names some owner exactly 96 times.
All inputs are finite; a program needn't handle non-finite values.
Results may differ from a plain program's by a relative error of at most 0.0065.
Values may be sent and summed in bfloat16 or wider, within the bound.
A program may use at most 64 MiB of HBM per device.

v0:
```python
import math
import jax
import jax.numpy as jnp
from jax import lax
from jax.sharding import PartitionSpec as P

OFFSETS = [(shift_lat, shift_lon) for shift_lat in (-1, 0, 1) for shift_lon in (-1, 0, 1)]


def extended(shard, sides, width):
    for axis, dim in sides:
        count, length = (lax.axis_size(axis), shard.shape[dim])
        up = [(i, (i + 1) % count) for i in range(count)]
        down = [(j, i) for i, j in up]
        last = lax.slice_in_dim(shard, length - width, length, axis=dim)
        first = lax.slice_in_dim(shard, 0, width, axis=dim)
        before = lax.ppermute(last, axis, up)
        after = lax.ppermute(first, axis, down)
        shard = jnp.concatenate([before, shard, after], axis=dim)
    return shard


def encoder(rows, weight_in, bias_in, weight_out):
    before = jnp.dot(rows, weight_in, preferred_element_type=jnp.float32) + bias_in
    hidden = jax.nn.gelu(before).astype(jnp.bfloat16)
    encoded = jnp.dot(hidden, weight_out, preferred_element_type=jnp.float32).astype(jnp.bfloat16)
    return (before, hidden, encoded)


def local_grads(rows, before, hidden, upstream, weight_out):
    contract = (((0,), (0,)), ((), ()))
    grad_out = lax.dot_general(hidden, upstream, contract, preferred_element_type=jnp.float32)
    back = lax.dot_general(
        upstream, weight_out, (((1,), (1,)), ((), ())), preferred_element_type=jnp.float32
    )
    _, pullback = jax.vjp(jax.nn.gelu, before)
    pre_grad = pullback(back)[0].astype(jnp.bfloat16)
    grad_in = lax.dot_general(rows, pre_grad, contract, preferred_element_type=jnp.float32)
    grad_bias = jnp.sum(pre_grad.astype(jnp.float32), axis=0)
    return (grad_in, grad_bias, grad_out)


def edge_mask(padded, tile_rows):
    lat_count = lax.axis_size("lat")
    lat_here = lax.axis_index("lat")
    row_ids = jnp.arange(tile_rows + 2, dtype=jnp.int32)
    outside = (row_ids == 0) & (lat_here == 0) | (row_ids == tile_rows + 1) & (
        lat_here == lat_count - 1
    )
    keep_rows = jnp.logical_not(outside).astype(padded.dtype)
    return padded * keep_rows[:, None, None]


def local(
    observations,
    owner_device,
    local_cell,
    valid_counts,
    weight_in,
    bias_in,
    weight_out,
    kernel_taps,
    cotangent,
):
    lat_count = lax.axis_size("lat")
    lon_count = lax.axis_size("lon")
    devices_all = lat_count * lon_count
    obs_rows = observations.shape[0]
    channels = weight_out.shape[1]
    capacity = 2 * obs_rows // devices_all
    tile_rows = cotangent.shape[0] * lon_count
    tile_cols = cotangent.shape[1] // lon_count
    cells_tile = tile_rows * tile_cols
    owners = owner_device[:, 0]
    valid_rows = jnp.arange(obs_rows, dtype=jnp.int32) < valid_counts[0]
    matches = (owners[:, None] == jnp.arange(devices_all, dtype=jnp.int32)[None, :]).astype(
        jnp.int32
    )
    earlier = jnp.sum((jnp.cumsum(matches, axis=0) - 1) * matches, axis=1)
    slot_index = owners * capacity + earlier
    sent_cells = jnp.full((devices_all * capacity,), cells_tile, jnp.int32)
    sent_cells = sent_cells.at[slot_index].set(jnp.where(valid_rows, local_cell, cells_tile))
    got_cells = lax.all_to_all(
        sent_cells.reshape(devices_all, capacity),
        ("lat", "lon"),
        split_axis=0,
        concat_axis=0,
        tiled=True,
    ).reshape(-1)
    width = observations.shape[1]
    outgoing = (
        jnp.zeros((devices_all * capacity, width), observations.dtype)
        .at[slot_index]
        .set(observations)
    )
    arrived = lax.all_to_all(
        outgoing.reshape(devices_all, capacity, width),
        ("lat", "lon"),
        split_axis=0,
        concat_axis=0,
        tiled=True,
    )
    arrived_rows = arrived.reshape(devices_all * capacity, width)
    before, hidden, arrived_enc = encoder(arrived_rows, weight_in, bias_in, weight_out)
    deposit = jax.ops.segment_sum(
        arrived_enc.astype(jnp.float32), got_cells, num_segments=cells_tile + 1
    )
    deposit = deposit[:cells_tile].reshape(tile_rows, tile_cols, channels)
    padded = extended(deposit, (("lat", 0), ("lon", 1)), 1)
    padded = edge_mask(padded, tile_rows)
    grid_field = jnp.zeros((tile_rows, tile_cols, channels), jnp.float32)
    for tap_index, (shift_lat, shift_lon) in enumerate(OFFSETS):
        window = padded[
            1 + shift_lat : 1 + shift_lat + tile_rows, 1 + shift_lon : 1 + shift_lon + tile_cols
        ]
        grid_field = grid_field + kernel_taps[tap_index] * window
    grid_out = lax.all_to_all(
        grid_field.astype(jnp.bfloat16), "lon", split_axis=0, concat_axis=1, tiled=True
    )
    loss_scale = 1.0 / math.sqrt(obs_rows * devices_all)
    cot_tile = lax.all_to_all(cotangent, "lon", split_axis=1, concat_axis=0, tiled=True)
    cot_float = cot_tile.astype(jnp.float32)
    cot_padded = extended(cot_tile, (("lat", 0), ("lon", 1)), 1)
    cot_padded = edge_mask(cot_padded, tile_rows).astype(jnp.float32)
    kernel_rows = []
    adjoint = jnp.zeros((tile_rows, tile_cols, channels), jnp.float32)
    for tap_index, (shift_lat, shift_lon) in enumerate(OFFSETS):
        window = padded[
            1 + shift_lat : 1 + shift_lat + tile_rows, 1 + shift_lon : 1 + shift_lon + tile_cols
        ]
        kernel_rows.append(loss_scale * jnp.sum(cot_float * window, axis=(0, 1)))
        back_window = cot_padded[
            1 - shift_lat : 1 - shift_lat + tile_rows, 1 - shift_lon : 1 - shift_lon + tile_cols
        ]
        adjoint = adjoint + kernel_taps[tap_index] * back_window
    grad_kernel = jnp.stack(kernel_rows)
    adjoint = (loss_scale * adjoint).astype(jnp.bfloat16)
    adjoint_rows = jnp.concatenate(
        [adjoint.reshape(cells_tile, channels), jnp.zeros((1, channels), jnp.bfloat16)], axis=0
    )
    upstream = adjoint_rows[got_cells]
    grads = local_grads(arrived_rows, before, hidden, upstream, weight_out)
    grad_in, grad_bias, grad_out, grad_kernel = lax.psum(
        (grads[0], grads[1], grads[2], grad_kernel), ("lat", "lon")
    )
    return (grid_out, grad_in, grad_bias, grad_out, grad_kernel)


def solution(mesh):
    return jax.shard_map(
        local,
        mesh=mesh,
        in_specs=(
            P(("lat", "lon"), None),
            P(("lat", "lon"), None),
            P(("lat", "lon")),
            P(("lat", "lon")),
            P(),
            P(),
            P(),
            P(),
            P(("lat", "lon"), None, None),
        ),
        out_specs=(P(("lat", "lon"), None, None), P(), P(), P(), P()),
        check_vma=False,
    )
```

profile of v0, /device:TPU:0, one launch (start us, length us, event | category | flops | bytes accessed | tf_op | source)
XLA Modules:
  0.0 271.2 jit_solution(18164300997538134326)
XLA Ops:
  7.9 0.7 reduce
  8.6 9.1 %reduce-window.6 = s32[32,12,128]{2,1,0:T(8,128)S(1)} reduce-window(s32[32,12,128]{2,1,0:T(8,128)S(1)} %fusion.30, s32[]{:T(128)} %constant.21.clone.1), window={size=1x1x128 pad=0_0x0_0x127_0}, to_apply=%region_0.0 | reduce-window | flops 6242304 | bytes 393220 | tf_op jit(solution)/shard_map/reduce-window
  17.7 0.1 slice.182
  17.8 0.2 copy.20
  18.1 0.1 copy.21
  18.2 0.1 add_add_fusion
  18.3 0.1 fusion.34
  18.4 0.7 fusion.36
  19.1 0.7 fusion.35
  19.8 6.2 %scatter_custom_fusion = s32[3072]{0:T(1024)S(1)} fusion(s32[1536]{0:T(1024)S(1)} %fusion.36, s32[1536]{0:T(1024)S(1)} %fusion.35, s32[]{:T(128)} %constant.19.clone.1), kind=kCustom, calls=%fused_computation.84 | custom fusion | bytes 12292 | tf_op jit(solution)/shard_map/scatter | solution.py:82
  26.0 0.7 all_to_all.35
  26.7 7.3 %all-to-all-start = ((s32[32,1,96]{2,1,0:T(1,128)}), s32[32,1,96]{2,1,0:T(1,128)S(1)}, u32[]{:S(2)}, u32[]{:S(2)}) async-start(s32[32,1,96]{2,1,0:T(1,128)} %all_to_all.35), calls=%async_computation | async-start | bytes 32768 | tf_op jit(solution)/shard_map/all_to_all | solution.py:83
  34.1 1.8 copy.23
  35.9 5.7 %scatter_custom_fusion.1 = bf16[3072,128]{1,0:T(8,128)(2,1)} fusion(s32[1536]{0:T(1024)S(1)} %fusion.36, bf16[1536,128]{1,0:T(8,128)(2,1)} %param.9, bf16[]{:T(256)} %constant.24.clone.1), kind=kCustom, calls=%fused_computation.57 | custom fusion | bytes 786944 | tf_op jit(solution)/shard_map/scatter | solution.py:94
  41.6 3.9 %all-to-all-start.3 = ((bf16[2,192,256]{2,0,1:T(2,128)(2,1)}), bf16[2,192,256]{2,0,1:T(2,128)(2,1)S(1)}, u32[]{:S(2)}, u32[]{:S(2)}) async-start(bf16[2,192,256]{2,0,1:T(2,128)(2,1)} %copy.23), calls=%async_computation.3 | async-start | bytes 393216 | tf_op jit(solution)/shard_map/all_to_all | solution.py:121
  45.6 0.1 broadcast_in_dim_reshape.3
  45.7 6.1 %all-to-all-done.3 = bf16[2,192,256]{2,0,1:T(2,128)(2,1)S(1)} async-done(((bf16[2,192,256]{2,0,1:T(2,128)(2,1)}), bf16[2,192,256]{2,0,1:T(2,128)(2,1)S(1)}, u32[]{:S(2)}, u32[]{:S(2)}) %all-to-all-start.3) | async-done | bytes 196640 | tf_op jit(solution)/shard_map/all_to_all | solution.py:121
  51.8 3.7 %all-to-all-start.1 = ((bf16[32,96,128]{2,1,0:T(8,128)(2,1)}), bf16[32,96,128]{2,1,0:T(8,128)(2,1)S(1)}, u32[]{:S(2)}, u32[]{:S(2)}) async-start(bf16[32,96,128]{2,1,0:T(8,128)(2,1)} %bitcast.4), calls=%async_computation.1 | async-start | bytes 1572864 | tf_op jit(solution)/shard_map/all_to_all | solution.py:96
  55.6 1.8 collective-permute-start.4
  57.4 2.1 collective-permute-start.5
  59.5 13.7 %collective-permute-done.4 = bf16[1,24,256]{2,1,0:T(8,128)(2,1)S(1)} collective-permute-done((bf16[1,24,256]{2,1,0:T(8,128)(2,1)S(1)}, bf16[1,24,256]{2,1,0:T(8,128)(2,1)S(1)}, u32[]{:S(2)}, u32[]{:S(2)}) %collective-permute-start.4) | collective-permute-done | bytes 12320 | tf_op jit(solution)/shard_map/ppermute | solution.py:17
  73.3 2.6 collective-permute-start.7
  76.0 0.5 broadcast.234
  76.5 0.7 reduce.9
  77.2 0.1 reshape.214
  77.2 0.2 collective-permute-done.6
  77.4 0.1 fusion.29
  77.6 0.3 fusion.19
  77.9 11.1 %gather_fusion = bf16[3072,256]{1,0:T(8,128)(2,1)S(1)} fusion(bf16[385,256]{1,0:T(8,128)(2,1)S(1)} %concatenate.19, s32[3072]{0:T(1024)S(1)} %broadcast_clamp_fusion), kind=kCustom, calls=%fused_computation | custom fusion | bytes 3158016 | tf_op jit(solution)/shard_map/gather | solution.py:141
  89.0 2.3 fusion.45
  91.3 5.0 %convert_reduce_fusion = (f32[256]{0:T(256)S(1)}, bf16[3072,256]{1,0:T(8,128)(2,1)}, f32[3072,256]{1,0:T(8,128)S(1)}) fusion(f32[3072,256]{1,0:T(8,128)} %fusion.45, f32[256]{0:T(256)S(1)} %copy-done.4, bf16[3072,128]{1,0:T(8,128)(2,1)S(1)} %bitcast.78, bf16[128,256]{1,0:T(8,128)(2,1)S(1)} %copy-done.3), kind=kOutput, calls=%fused_computation.16 | convolution fusion | flops 219414272 | bytes 8718336 | tf_op jit(solution)/shard_map/dot_general | solution.py:24
  96.2 1.7 copy-done.5
  97.9 2.8 %fusion = f32[3072,256]{1,0:T(8,128)} fusion(bf16[256,256]{1,0:T(8,128)(2,1)S(1)} %copy-done, f32[3072,256]{1,0:T(8,128)S(1)} %get-tuple-element.37), kind=kOutput, calls=%fused_computation.8 | convolution fusion | flops 411303936 | bytes 6422528 | tf_op jit(solution)/shard_map/dot_general | solution.py:26
  100.7 19.6 %scatter_custom_fusion.2 = f32[385,256]{1,0:T(8,128)S(1)} fusion(s32[3072]{0:T(1024)S(1)} %reshape.214, f32[3072,256]{1,0:T(8,128)} %fusion, f32[]{:T(128)} %constant.18.clone.1), kind=kCustom, calls=%fused_computation.64 | custom fusion | flops 786432 | bytes 394752 | tf_op jit(solution)/shard_map/scatter-add | solution.py:105
  120.4 4.8 %collective-permute-start = (f32[1,24,256]{2,1,0:T(8,128)S(1)}, f32[1,24,256]{2,1,0:T(8,128)S(1)}, u32[]{:S(2)}, u32[]{:S(2)}) collective-permute-start(f32[1,24,256]{2,1,0:T(8,128)S(1)} %get-tuple-element.22), channel_id=1, source_target_pairs={{0,8},{8,16},{16,24},{24,0},{1,9},{9,17},{17,25},{25,1},{2,10},{10... | collective-permute-start | bytes 73736 | tf_op jit(solution)/shard_map/ppermute | solution.py:17
  125.2 3.9 %fusion.41 = f32[256,256]{1,0:T(8,128)} fusion(bf16[3072,256]{1,0:T(8,128)(2,1)S(1)} %gather_fusion, f32[3072,256]{1,0:T(8,128)} %copy-done.5), kind=kOutput, calls=%fused_computation.98 | convolution fusion | flops 409731072 | bytes 4980736 | tf_op jit(solution)/shard_map/dot_general | solution.py:32
  129.2 2.6 collective-permute-start.3
  131.9 1.1 fusion.46
  133.0 0.3 collective-permute-done.2
  133.3 0.1 maximum_multiply_fusion
  133.4 0.3 fusion.16
  133.8 1.0 add_convert_fusion
  134.7 3.9 %all-to-all-start.2 = ((bf16[16,24,256]{2,1,0:T(8,128)(2,1)}), bf16[16,24,256]{2,1,0:T(8,128)(2,1)S(1)}, u32[]{:S(2)}, u32[]{:S(2)}) async-start(bf16[16,24,256]{2,1,0:T(8,128)(2,1)} %add_convert_fusion), calls=%async_computation.2 | async-start | bytes 393216 | tf_op jit(solution)/shard_map/all_to_all | solution.py:117
  138.7 41.4 %all-reduce.1 = (f32[256]{0:T(256)}, f32[9,256]{1,0:T(8,128)}) all-reduce(f32[256]{0:T(256)S(1)} %get-tuple-element.18, f32[9,256]{1,0:T(8,128)S(1)} %stack.2), channel_id=1, replica_groups=mesh['lat'=4,'lon'=8] {'lat','lon'}, use_global_device_ids=true, to_apply=%region_8.9 | all-reduce | flops 2560 | bytes 20480 | tf_op jit(solution)/shard_map/psum | solution.py:143
  180.2 0.7 copy.22
  180.9 80.2 %all-reduce.5.cloned.1.call-done = (f32[128,256]{1,0:T(8,128)}, f32[256,256]{1,0:T(8,128)}) async-done(((f32[128,256]{1,0:T(8,128)}, f32[256,256]{1,0:T(8,128)}), (f32[128,256]{1,0:T(8,128)}, f32[256,256]{1,0:T(8,128)})) %all-reduce.5.cloned.1.call-update) | async-done | bytes 393232 | tf_op jit(solution)/shard_map/psum | solution.py:143
  261.1 1.6 copy.30
  262.7 1.7 copy.31
  (44 shorter events, 0.6 us)
Async XLA Ops:
  7.2 81.8 %copy-start = (bf16[256,256]{1,0:T(8,128)(2,1)S(1)}, bf16[256,256]{1,0:T(8,128)(2,1)}, u32[]{:S(2)}) copy-start(bf16[256,256]{1,0:T(8,128)(2,1)} %param.15) | copy-start | bytes 393220
  7.2 38.4 %copy-start.2 = (f32[9,256]{1,0:T(8,128)S(1)}, f32[9,256]{1,0:T(8,128)}, u32[]{:S(2)}) copy-start(f32[9,256]{1,0:T(8,128)} %param.16) | copy-start | bytes 27652
  26.7 14.9 %all-to-all-start = ((s32[32,1,96]{2,1,0:T(1,128)}), s32[32,1,96]{2,1,0:T(1,128)S(1)}, u32[]{:S(2)}, u32[]{:S(2)}) async-start(s32[32,1,96]{2,1,0:T(1,128)} %all_to_all.35), calls=%async_computation | async-start | bytes 32768 | tf_op jit(solution)/shard_map/all_to_all | solution.py:83
  41.6 10.1 %all-to-all-start.3 = ((bf16[2,192,256]{2,0,1:T(2,128)(2,1)}), bf16[2,192,256]{2,0,1:T(2,128)(2,1)S(1)}, u32[]{:S(2)}, u32[]{:S(2)}) async-start(bf16[2,192,256]{2,0,1:T(2,128)(2,1)} %copy.23), calls=%async_computation.3 | async-start | bytes 393216 | tf_op jit(solution)/shard_map/all_to_all | solution.py:121
  51.8 39.5 %all-to-all-start.1 = ((bf16[32,96,128]{2,1,0:T(8,128)(2,1)}), bf16[32,96,128]{2,1,0:T(8,128)(2,1)S(1)}, u32[]{:S(2)}, u32[]{:S(2)}) async-start(bf16[32,96,128]{2,1,0:T(8,128)(2,1)} %bitcast.4), calls=%async_computation.1 | async-start | bytes 1572864 | tf_op jit(solution)/shard_map/all_to_all | solution.py:96
  55.5 205.6 %all-reduce.5.cloned.1.call-start = ((), (), s32[]{:S(2)}) async-start(), calls=%async_computation.4 | async-start | bytes 786432 | tf_op jit(solution)/shard_map/psum | solution.py:143
  55.6 17.6 %collective-permute-start.4 = (bf16[1,24,256]{2,1,0:T(8,128)(2,1)S(1)}, bf16[1,24,256]{2,1,0:T(8,128)(2,1)S(1)}, u32[]{:S(2)}, u32[]{:S(2)}) collective-permute-start(bf16[1,24,256]{2,1,0:T(8,128)(2,1)S(1)} %get-tuple-element.26), channel_id=1, source_target_pairs={{0,8},{8,16},{16,24},{24,0},{1,9},{9,17},{17,25},{25,1},{2,10},{10... | collective-permute-start | bytes 36872 | tf_op jit(solution)/shard_map/ppermute | solution.py:17
  57.4 15.8 %collective-permute-start.5 = (bf16[1,24,256]{2,1,0:T(8,128)(2,1)S(1)}, bf16[1,24,256]{2,1,0:T(8,128)(2,1)S(1)}, u32[]{:S(2)}, u32[]{:S(2)}) collective-permute-start(bf16[1,24,256]{2,1,0:T(8,128)(2,1)S(1)} %get-tuple-element.27), channel_id=1, source_target_pairs={{8,0},{16,8},{24,16},{0,24},{9,1},{17,9},{25,17},{1,25},{10,2},{18... | collective-permute-start | bytes 36872 | tf_op jit(solution)/shard_map/ppermute | solution.py:18
  73.3 4.1 %collective-permute-start.6 = (bf16[18,1,256]{2,1,0:T(2,128)(2,1)S(1)}, bf16[18,1,256]{2,1,0:T(2,128)(2,1)S(1)}, u32[]{:S(2)}, u32[]{:S(2)}) collective-permute-start(bf16[18,1,256]{2,1,0:T(2,128)(2,1)S(1)} %get-tuple-element.24), channel_id=1, source_target_pairs={{0,1},{1,2},{2,3},{3,4},{4,5},{5,6},{6,7},{7,0},{8,9},{9,10},{10,1... | collective-permute-start | bytes 27656 | tf_op jit(solution)/shard_map/ppermute | solution.py:17
  73.3 4.1 %collective-permute-start.7 = (bf16[18,1,256]{2,1,0:T(2,128)(2,1)S(1)}, bf16[18,1,256]{2,1,0:T(2,128)(2,1)S(1)}, u32[]{:S(2)}, u32[]{:S(2)}) collective-permute-start(bf16[18,1,256]{2,1,0:T(2,128)(2,1)S(1)} %get-tuple-element.25), channel_id=1, source_target_pairs={{1,0},{2,1},{3,2},{4,3},{5,4},{6,5},{7,6},{0,7},{9,8},{10,9},{11,1... | collective-permute-start | bytes 27656 | tf_op jit(solution)/shard_map/ppermute | solution.py:18
  89.0 2.3 copy-start.3
  89.0 2.3 copy-start.4
  96.2 1.7 copy-start.5
  120.4 8.7 %collective-permute-start = (f32[1,24,256]{2,1,0:T(8,128)S(1)}, f32[1,24,256]{2,1,0:T(8,128)S(1)}, u32[]{:S(2)}, u32[]{:S(2)}) collective-permute-start(f32[1,24,256]{2,1,0:T(8,128)S(1)} %get-tuple-element.22), channel_id=1, source_target_pairs={{0,8},{8,16},{16,24},{24,0},{1,9},{9,17},{17,25},{25,1},{2,10},{10... | collective-permute-start | bytes 73736 | tf_op jit(solution)/shard_map/ppermute | solution.py:17
  125.2 6.7 %copy-start.1 = (bf16[3072,256]{1,0:T(8,128)(2,1)S(1)}, bf16[3072,256]{1,0:T(8,128)(2,1)}, u32[]{:S(2)}) copy-start(bf16[3072,256]{1,0:T(8,128)(2,1)} %get-tuple-element.19) | copy-start | bytes 4718596
  125.2 3.9 %collective-permute-start.1 = (f32[1,24,256]{2,1,0:T(8,128)S(1)}, f32[1,24,256]{2,1,0:T(8,128)S(1)}, u32[]{:S(2)}, u32[]{:S(2)}) collective-permute-start(f32[1,24,256]{2,1,0:T(8,128)S(1)} %get-tuple-element.23), channel_id=1, source_target_pairs={{8,0},{16,8},{24,16},{0,24},{9,1},{17,9},{25,17},{1,25},{10,2},{18... | collective-permute-start | bytes 73736 | tf_op jit(solution)/shard_map/ppermute | solution.py:18
  129.2 4.1 %collective-permute-start.2 = (f32[18,1,256]{2,1,0:T(1,128)S(1)}, f32[18,1,256]{2,1,0:T(1,128)S(1)}, u32[]{:S(2)}, u32[]{:S(2)}) collective-permute-start(f32[18,1,256]{2,1,0:T(1,128)S(1)} %get-tuple-element.20), channel_id=1, source_target_pairs={{0,1},{1,2},{2,3},{3,4},{4,5},{5,6},{6,7},{7,0},{8,9},{9,10},{10,1... | collective-permute-start | bytes 55304 | tf_op jit(solution)/shard_map/ppermute | solution.py:17
  129.2 4.1 %collective-permute-start.3 = (f32[18,1,256]{2,1,0:T(1,128)S(1)}, f32[18,1,256]{2,1,0:T(1,128)S(1)}, u32[]{:S(2)}, u32[]{:S(2)}) collective-permute-start(f32[18,1,256]{2,1,0:T(1,128)S(1)} %get-tuple-element.21), channel_id=1, source_target_pairs={{1,0},{2,1},{3,2},{4,3},{5,4},{6,5},{7,6},{0,7},{9,8},{10,9},{11,1... | collective-permute-start | bytes 55304 | tf_op jit(solution)/shard_map/ppermute | solution.py:18
  134.7 45.4 %all-to-all-start.2 = ((bf16[16,24,256]{2,1,0:T(8,128)(2,1)}), bf16[16,24,256]{2,1,0:T(8,128)(2,1)S(1)}, u32[]{:S(2)}, u32[]{:S(2)}) async-start(bf16[16,24,256]{2,1,0:T(8,128)(2,1)} %add_convert_fusion), calls=%async_computation.2 | async-start | bytes 393216 | tf_op jit(solution)/shard_map/all_to_all | solution.py:117
Sparse Core Ops, SparseCore 0:
  133.1 127.9 all-reduce.4
where the time goes:
time: 272 us; the launch traced here: 271 us
  waiting for transfers between devices  101 us (37%)
  blocking collectives  41.4 us (15%)
  other arithmetic  33.8 us (12%)
  starting transfers between devices  33 us (12%)
  local copies, waits for them, and re-layouts  32.3 us (12%)
  matrix products  15 us (6%)
  between operations  15 us (6%)
    psum x1, waiting for transfers between devices, local(): lax.psum((grads[0], grads[1], grads[2], grad_kernel), ('lat', 'lon'))  80.2 us
    psum x1, blocking collectives, local(): lax.psum((grads[0], grads[1], grads[2], grad_kernel), ('lat', 'lon'))  41.4 us
    scatter-add x1, other arithmetic, local(): jax.ops.segment_sum(arrived_enc.astype(jnp.float32), got_cells, num_segme...  19.6 us
    ppermute x4, waiting for transfers between devices, extended(): before = lax.ppermute(last, axis, up)  14.2 us
    gather x1, local copies, waits for them, and re-layouts, local(): upstream = adjoint_rows[got_cells]  11.1 us
    another operation x2, other arithmetic  9.11 us
    all_to_all x1, starting transfers between devices, local(): lax.all_to_all(sent_cells.reshape(devices_all, capacity), ('lat', 'lon'),...  7.33 us
    ppermute x4, starting transfers between devices, extended(): after = lax.ppermute(first, axis, down)  7.32 us
  transfers between devices with their start and end apart: 13, of which 5 were waited for; matrix products, arithmetic and copies ran while one was open for 11% of the time, Pallas kernels for 0%

commit v1 on v0

--- a/solution.py
+++ b/solution.py
@@ -3,6 +3,7 @@
 import jax.numpy as jnp
 from jax import lax
 from jax.sharding import PartitionSpec as P
+from jax.lax import psum
 
 OFFSETS = [(shift_lat, shift_lon) for shift_lat in (-1, 0, 1) for shift_lon in (-1, 0, 1)]
 
@@ -140,8 +141,8 @@
     )
     upstream = adjoint_rows[got_cells]
     grads = local_grads(arrived_rows, before, hidden, upstream, weight_out)
-    grad_in, grad_bias, grad_out, grad_kernel = lax.psum(
-        (grads[0], grads[1], grads[2], grad_kernel), ("lat", "lon")
+    grad_in, grad_bias, grad_out, grad_kernel = psum(
+        psum((grads[0], grads[1], grads[2], grad_kernel), "lon"), "lat"
     )
     return (grid_out, grad_in, grad_bias, grad_out, grad_kernel)
 

time: 272 us -> 241 us (0.89)
  waiting for transfers between devices: 101 us -> 68.3 us
    psum x1 -> x2, waiting for transfers between devices: 80.2 us -> 47.9 us  [the longest x1 47.9 us: local(): psum((grads[0], grads[1], grads[2], grad_kernel), 'lon')]
    psum x1 -> x2, blocking collectives: 41.4 us -> 42.5 us  [the longest x1 22.4 us: local(): psum((grads[0], grads[1], grads[2], grad_kernel), 'lon')]
  transfers between devices with their start and end apart: 13 -> 14, of which waited for: 5 -> 5; matrix products, arithmetic and copies ran while one was open for 11% -> 12% of each run, Pallas kernels for 0% -> 0%
where the time goes in v1:
time: 241 us; the launch traced here: 240 us
  waiting for transfers between devices  68.3 us (28%)
  blocking collectives  42.5 us (18%)
  other arithmetic  33.8 us (14%)
  starting transfers between devices  33 us (14%)
  local copies, waits for them, and re-layouts  32.3 us (13%)
  matrix products  15 us (6%)
  between operations  15 us (6%)
    psum x1, waiting for transfers between devices, local(): psum((grads[0], grads[1], grads[2], grad_kernel), 'lon')  47.9 us
    psum x1, blocking collectives, local(): psum((grads[0], grads[1], grads[2], grad_kernel), 'lon')  22.4 us
    psum x1, blocking collectives, local(): psum(psum((grads[0], grads[1], grads[2], grad_kernel), 'lon'), 'lat')  20.1 us
    scatter-add x1, other arithmetic, local(): jax.ops.segment_sum(arrived_enc.astype(jnp.float32), got_cells, num_segme...  19.6 us
    ppermute x4, waiting for transfers between devices, extended(): before = lax.ppermute(last, axis, up)  14.2 us
    gather x1, local copies, waits for them, and re-layouts, local(): upstream = adjoint_rows[got_cells]  11.1 us
    another operation x2, other arithmetic  9.11 us
    all_to_all x1, starting transfers between devices, local(): lax.all_to_all(sent_cells.reshape(devices_all, capacity), ('lat', 'lon'),...  7.33 us
  transfers between devices with their start and end apart: 14, of which 5 were waited for; matrix products, arithmetic and copies ran while one was open for 12% of the time, Pallas kernels for 0%

profile of v1, /device:TPU:0, one launch (start us, length us, event | category | flops | bytes accessed | tf_op | source)
XLA Modules:
  0.0 240.0 jit_solution(10202258912781663699)
XLA Ops:
  7.9 0.7 reduce
  8.6 9.1 %reduce-window.6 = s32[32,12,128]{2,1,0:T(8,128)S(1)} reduce-window(s32[32,12,128]{2,1,0:T(8,128)S(1)} %fusion.30, s32[]{:T(128)} %constant.21.clone.1), window={size=1x1x128 pad=0_0x0_0x127_0}, to_apply=%region_0.0 | reduce-window | flops 6242304 | bytes 393220 | tf_op jit(solution)/shard_map/reduce-window
  17.7 0.1 slice.182
  17.8 0.2 copy.20
  18.1 0.1 copy.21
  18.2 0.1 add_add_fusion
  18.3 0.1 fusion.34
  18.4 0.7 fusion.36
  19.1 0.7 fusion.35
  19.8 6.2 %scatter_custom_fusion = s32[3072]{0:T(1024)S(1)} fusion(s32[1536]{0:T(1024)S(1)} %fusion.36, s32[1536]{0:T(1024)S(1)} %fusion.35, s32[]{:T(128)} %constant.19.clone.1), kind=kCustom, calls=%fused_computation.84 | custom fusion | bytes 12292 | tf_op jit(solution)/shard_map/scatter | solution.py:83
  26.0 0.7 all_to_all.35
  26.7 7.3 %all-to-all-start = ((s32[32,1,96]{2,1,0:T(1,128)}), s32[32,1,96]{2,1,0:T(1,128)S(1)}, u32[]{:S(2)}, u32[]{:S(2)}) async-start(s32[32,1,96]{2,1,0:T(1,128)} %all_to_all.35), calls=%async_computation | async-start | bytes 32768 | tf_op jit(solution)/shard_map/all_to_all | solution.py:84
  34.1 1.8 copy.23
  35.9 5.7 %scatter_custom_fusion.1 = bf16[3072,128]{1,0:T(8,128)(2,1)} fusion(s32[1536]{0:T(1024)S(1)} %fusion.36, bf16[1536,128]{1,0:T(8,128)(2,1)} %param.9, bf16[]{:T(256)} %constant.24.clone.1), kind=kCustom, calls=%fused_computation.57 | custom fusion | bytes 786944 | tf_op jit(solution)/shard_map/scatter | solution.py:95
  41.6 3.9 %all-to-all-start.3 = ((bf16[2,192,256]{2,0,1:T(2,128)(2,1)}), bf16[2,192,256]{2,0,1:T(2,128)(2,1)S(1)}, u32[]{:S(2)}, u32[]{:S(2)}) async-start(bf16[2,192,256]{2,0,1:T(2,128)(2,1)} %copy.23), calls=%async_computation.3 | async-start | bytes 393216 | tf_op jit(solution)/shard_map/all_to_all | solution.py:122
  45.6 0.1 broadcast_in_dim_reshape.3
  45.7 6.1 %all-to-all-done.3 = bf16[2,192,256]{2,0,1:T(2,128)(2,1)S(1)} async-done(((bf16[2,192,256]{2,0,1:T(2,128)(2,1)}), bf16[2,192,256]{2,0,1:T(2,128)(2,1)S(1)}, u32[]{:S(2)}, u32[]{:S(2)}) %all-to-all-start.3) | async-done | bytes 196640 | tf_op jit(solution)/shard_map/all_to_all | solution.py:122
  51.8 3.7 %all-to-all-start.1 = ((bf16[32,96,128]{2,1,0:T(8,128)(2,1)}), bf16[32,96,128]{2,1,0:T(8,128)(2,1)S(1)}, u32[]{:S(2)}, u32[]{:S(2)}) async-start(bf16[32,96,128]{2,1,0:T(8,128)(2,1)} %bitcast.4), calls=%async_computation.1 | async-start | bytes 1572864 | tf_op jit(solution)/shard_map/all_to_all | solution.py:97
  55.6 1.8 collective-permute-start.4
  57.4 2.1 collective-permute-start.5
  59.5 13.7 %collective-permute-done.4 = bf16[1,24,256]{2,1,0:T(8,128)(2,1)S(1)} collective-permute-done((bf16[1,24,256]{2,1,0:T(8,128)(2,1)S(1)}, bf16[1,24,256]{2,1,0:T(8,128)(2,1)S(1)}, u32[]{:S(2)}, u32[]{:S(2)}) %collective-permute-start.4) | collective-permute-done | bytes 12320 | tf_op jit(solution)/shard_map/ppermute | solution.py:18
  73.3 2.6 %collective-permute-start.7 = (bf16[18,1,256]{2,1,0:T(2,128)(2,1)S(1)}, bf16[18,1,256]{2,1,0:T(2,128)(2,1)S(1)}, u32[]{:S(2)}, u32[]{:S(2)}) collective-permute-start(bf16[18,1,256]{2,1,0:T(2,128)(2,1)S(1)} %get-tuple-element.29), channel_id=1, source_target_pairs={{1,0},{2,1},{3,2},{4,3},{5,4},{6,5},{7,6},{0,7},{9,8},{10,9},{11,1... | collective-permute-start | bytes 27656 | tf_op jit(solution)/shard_map/ppermute | solution.py:19
  76.0 0.5 broadcast.234
  76.5 0.7 reduce.9
  77.3 0.2 collective-permute-done.6
  77.4 0.1 fusion.29
  77.6 0.3 fusion.19
  77.9 11.1 %gather_fusion = bf16[3072,256]{1,0:T(8,128)(2,1)S(1)} fusion(bf16[385,256]{1,0:T(8,128)(2,1)S(1)} %concatenate.19, s32[3072]{0:T(1024)S(1)} %broadcast_clamp_fusion), kind=kCustom, calls=%fused_computation | custom fusion | bytes 3158016 | tf_op jit(solution)/shard_map/gather | solution.py:142
  89.0 2.3 fusion.45
  91.3 5.0 %convert_reduce_fusion = (f32[256]{0:T(256)S(1)}, bf16[3072,256]{1,0:T(8,128)(2,1)}, f32[3072,256]{1,0:T(8,128)S(1)}) fusion(f32[3072,256]{1,0:T(8,128)} %fusion.45, f32[256]{0:T(256)S(1)} %copy-done.4, bf16[3072,128]{1,0:T(8,128)(2,1)S(1)} %bitcast.78, bf16[128,256]{1,0:T(8,128)(2,1)S(1)} %copy-done.3), kind=kOutput, calls=%fused_computation.16 | convolution fusion | flops 219414272 | bytes 8718336 | tf_op jit(solution)/shard_map/dot_general | solution.py:25
  96.2 1.7 copy-done.5
  97.9 2.8 %fusion = f32[3072,256]{1,0:T(8,128)} fusion(bf16[256,256]{1,0:T(8,128)(2,1)S(1)} %copy-done, f32[3072,256]{1,0:T(8,128)S(1)} %get-tuple-element.41), kind=kOutput, calls=%fused_computation.8 | convolution fusion | flops 411303936 | bytes 6422528 | tf_op jit(solution)/shard_map/dot_general | solution.py:27
  100.7 19.6 %scatter_custom_fusion.2 = f32[385,256]{1,0:T(8,128)S(1)} fusion(s32[3072]{0:T(1024)S(1)} %reshape.214, f32[3072,256]{1,0:T(8,128)} %fusion, f32[]{:T(128)} %constant.18.clone.1), kind=kCustom, calls=%fused_computation.64 | custom fusion | flops 786432 | bytes 394752 | tf_op jit(solution)/shard_map/scatter-add | solution.py:106
  120.4 4.8 %collective-permute-start = (f32[1,24,256]{2,1,0:T(8,128)S(1)}, f32[1,24,256]{2,1,0:T(8,128)S(1)}, u32[]{:S(2)}, u32[]{:S(2)}) collective-permute-start(f32[1,24,256]{2,1,0:T(8,128)S(1)} %get-tuple-element.26), channel_id=1, source_target_pairs={{0,8},{8,16},{16,24},{24,0},{1,9},{9,17},{17,25},{25,1},{2,10},{10... | collective-permute-start | bytes 73736 | tf_op jit(solution)/shard_map/ppermute | solution.py:18
  125.2 3.9 %fusion.41 = f32[256,256]{1,0:T(8,128)} fusion(bf16[3072,256]{1,0:T(8,128)(2,1)S(1)} %gather_fusion, f32[3072,256]{1,0:T(8,128)} %copy-done.5), kind=kOutput, calls=%fused_computation.98 | convolution fusion | flops 409731072 | bytes 4980736 | tf_op jit(solution)/shard_map/dot_general | solution.py:33
  129.2 2.6 %collective-permute-start.3 = (f32[18,1,256]{2,1,0:T(1,128)S(1)}, f32[18,1,256]{2,1,0:T(1,128)S(1)}, u32[]{:S(2)}, u32[]{:S(2)}) collective-permute-start(f32[18,1,256]{2,1,0:T(1,128)S(1)} %get-tuple-element.25), channel_id=1, source_target_pairs={{1,0},{2,1},{3,2},{4,3},{5,4},{6,5},{7,6},{0,7},{9,8},{10,9},{11,1... | collective-permute-start | bytes 55304 | tf_op jit(solution)/shard_map/ppermute | solution.py:19
  131.8 1.1 fusion.46
  133.0 0.3 collective-permute-done.2
  133.3 0.1 maximum_multiply_fusion
  133.4 0.3 fusion.16
  133.8 1.0 add_convert_fusion
  134.7 3.9 %all-to-all-start.2 = ((bf16[16,24,256]{2,1,0:T(8,128)(2,1)}), bf16[16,24,256]{2,1,0:T(8,128)(2,1)S(1)}, u32[]{:S(2)}, u32[]{:S(2)}) async-start(bf16[16,24,256]{2,1,0:T(8,128)(2,1)} %add_convert_fusion), calls=%async_computation.2 | async-start | bytes 393216 | tf_op jit(solution)/shard_map/all_to_all | solution.py:118
  138.7 47.9 %all-reduce.8.cloned.1.call-done = (f32[128,256]{1,0:T(8,128)}, f32[256,256]{1,0:T(8,128)}) async-done(((f32[128,256]{1,0:T(8,128)}, f32[256,256]{1,0:T(8,128)}), (f32[128,256]{1,0:T(8,128)}, f32[256,256]{1,0:T(8,128)})) %all-reduce.8.cloned.1.call-update) | async-done | bytes 393232 | tf_op jit(solution)/shard_map/psum | solution.py:145
  186.7 22.4 %all-reduce.1 = (f32[256]{0:T(256)S(1)}, f32[9,256]{1,0:T(8,128)S(1)}) all-reduce(f32[256]{0:T(256)S(1)} %get-tuple-element.22, f32[9,256]{1,0:T(8,128)S(1)} %stack.2), channel_id=1, replica_groups=mesh['lat'=4,'lon'=8] {'lon'}, use_global_device_ids=true, to_apply=%region_9.10 | all-reduce | flops 2560 | bytes 20480 | tf_op jit(solution)/shard_map/psum | solution.py:145
  209.1 20.1 %all-reduce.3 = (f32[256]{0:T(256)}, f32[9,256]{1,0:T(8,128)}) all-reduce(f32[256]{0:T(256)S(1)} %get-tuple-element.14, f32[9,256]{1,0:T(8,128)S(1)} %get-tuple-element.15), channel_id=1, replica_groups=mesh['lat'=4,'lon'=8] {'lat'}, use_global_device_ids=true, to_apply=%region_10.11 | all-reduce | flops 2560 | bytes 20480 | tf_op jit(solution)/shard_map/psum | solution.py:144
  229.2 0.7 copy.22
  229.9 1.6 copy.32
  231.5 1.7 copy.33
  (48 shorter events, 0.7 us)
Async XLA Ops:
  7.2 81.8 %copy-start = (bf16[256,256]{1,0:T(8,128)(2,1)S(1)}, bf16[256,256]{1,0:T(8,128)(2,1)}, u32[]{:S(2)}) copy-start(bf16[256,256]{1,0:T(8,128)(2,1)} %param.15) | copy-start | bytes 393220
  7.2 38.4 %copy-start.2 = (f32[9,256]{1,0:T(8,128)S(1)}, f32[9,256]{1,0:T(8,128)}, u32[]{:S(2)}) copy-start(f32[9,256]{1,0:T(8,128)} %param.16) | copy-start | bytes 27652
  26.7 14.9 %all-to-all-start = ((s32[32,1,96]{2,1,0:T(1,128)}), s32[32,1,96]{2,1,0:T(1,128)S(1)}, u32[]{:S(2)}, u32[]{:S(2)}) async-start(s32[32,1,96]{2,1,0:T(1,128)} %all_to_all.35), calls=%async_computation | async-start | bytes 32768 | tf_op jit(solution)/shard_map/all_to_all | solution.py:84
  41.6 10.1 %all-to-all-start.3 = ((bf16[2,192,256]{2,0,1:T(2,128)(2,1)}), bf16[2,192,256]{2,0,1:T(2,128)(2,1)S(1)}, u32[]{:S(2)}, u32[]{:S(2)}) async-start(bf16[2,192,256]{2,0,1:T(2,128)(2,1)} %copy.23), calls=%async_computation.3 | async-start | bytes 393216 | tf_op jit(solution)/shard_map/all_to_all | solution.py:122
  51.8 39.5 %all-to-all-start.1 = ((bf16[32,96,128]{2,1,0:T(8,128)(2,1)}), bf16[32,96,128]{2,1,0:T(8,128)(2,1)S(1)}, u32[]{:S(2)}, u32[]{:S(2)}) async-start(bf16[32,96,128]{2,1,0:T(8,128)(2,1)} %bitcast.4), calls=%async_computation.1 | async-start | bytes 1572864 | tf_op jit(solution)/shard_map/all_to_all | solution.py:97
  55.5 131.1 %all-reduce.8.cloned.1.call-start = ((), (), s32[]{:S(2)}) async-start(), calls=%async_computation.4 | async-start | bytes 786432 | tf_op jit(solution)/shard_map/psum | solution.py:145
  55.6 17.6 %collective-permute-start.4 = (bf16[1,24,256]{2,1,0:T(8,128)(2,1)S(1)}, bf16[1,24,256]{2,1,0:T(8,128)(2,1)S(1)}, u32[]{:S(2)}, u32[]{:S(2)}) collective-permute-start(bf16[1,24,256]{2,1,0:T(8,128)(2,1)S(1)} %get-tuple-element.30), channel_id=1, source_target_pairs={{0,8},{8,16},{16,24},{24,0},{1,9},{9,17},{17,25},{25,1},{2,10},{10... | collective-permute-start | bytes 36872 | tf_op jit(solution)/shard_map/ppermute | solution.py:18
  57.4 15.8 %collective-permute-start.5 = (bf16[1,24,256]{2,1,0:T(8,128)(2,1)S(1)}, bf16[1,24,256]{2,1,0:T(8,128)(2,1)S(1)}, u32[]{:S(2)}, u32[]{:S(2)}) collective-permute-start(bf16[1,24,256]{2,1,0:T(8,128)(2,1)S(1)} %get-tuple-element.31), channel_id=1, source_target_pairs={{8,0},{16,8},{24,16},{0,24},{9,1},{17,9},{25,17},{1,25},{10,2},{18... | collective-permute-start | bytes 36872 | tf_op jit(solution)/shard_map/ppermute | solution.py:19
  73.3 4.1 %collective-permute-start.6 = (bf16[18,1,256]{2,1,0:T(2,128)(2,1)S(1)}, bf16[18,1,256]{2,1,0:T(2,128)(2,1)S(1)}, u32[]{:S(2)}, u32[]{:S(2)}) collective-permute-start(bf16[18,1,256]{2,1,0:T(2,128)(2,1)S(1)} %get-tuple-element.28), channel_id=1, source_target_pairs={{0,1},{1,2},{2,3},{3,4},{4,5},{5,6},{6,7},{7,0},{8,9},{9,10},{10,1... | collective-permute-start | bytes 27656 | tf_op jit(solution)/shard_map/ppermute | solution.py:18
  73.3 4.1 %collective-permute-start.7 = (bf16[18,1,256]{2,1,0:T(2,128)(2,1)S(1)}, bf16[18,1,256]{2,1,0:T(2,128)(2,1)S(1)}, u32[]{:S(2)}, u32[]{:S(2)}) collective-permute-start(bf16[18,1,256]{2,1,0:T(2,128)(2,1)S(1)} %get-tuple-element.29), channel_id=1, source_target_pairs={{1,0},{2,1},{3,2},{4,3},{5,4},{6,5},{7,6},{0,7},{9,8},{10,9},{11,1... | collective-permute-start | bytes 27656 | tf_op jit(solution)/shard_map/ppermute | solution.py:19
  89.0 2.3 copy-start.3
  89.0 2.3 copy-start.4
  96.2 1.7 copy-start.5
  120.4 8.7 %collective-permute-start = (f32[1,24,256]{2,1,0:T(8,128)S(1)}, f32[1,24,256]{2,1,0:T(8,128)S(1)}, u32[]{:S(2)}, u32[]{:S(2)}) collective-permute-start(f32[1,24,256]{2,1,0:T(8,128)S(1)} %get-tuple-element.26), channel_id=1, source_target_pairs={{0,8},{8,16},{16,24},{24,0},{1,9},{9,17},{17,25},{25,1},{2,10},{10... | collective-permute-start | bytes 73736 | tf_op jit(solution)/shard_map/ppermute | solution.py:18
  125.2 6.7 %copy-start.1 = (bf16[3072,256]{1,0:T(8,128)(2,1)S(1)}, bf16[3072,256]{1,0:T(8,128)(2,1)}, u32[]{:S(2)}) copy-start(bf16[3072,256]{1,0:T(8,128)(2,1)} %get-tuple-element.23) | copy-start | bytes 4718596
  125.2 3.9 %collective-permute-start.1 = (f32[1,24,256]{2,1,0:T(8,128)S(1)}, f32[1,24,256]{2,1,0:T(8,128)S(1)}, u32[]{:S(2)}, u32[]{:S(2)}) collective-permute-start(f32[1,24,256]{2,1,0:T(8,128)S(1)} %get-tuple-element.27), channel_id=1, source_target_pairs={{8,0},{16,8},{24,16},{0,24},{9,1},{17,9},{25,17},{1,25},{10,2},{18... | collective-permute-start | bytes 73736 | tf_op jit(solution)/shard_map/ppermute | solution.py:19
  129.1 4.1 %collective-permute-start.2 = (f32[18,1,256]{2,1,0:T(1,128)S(1)}, f32[18,1,256]{2,1,0:T(1,128)S(1)}, u32[]{:S(2)}, u32[]{:S(2)}) collective-permute-start(f32[18,1,256]{2,1,0:T(1,128)S(1)} %get-tuple-element.24), channel_id=1, source_target_pairs={{0,1},{1,2},{2,3},{3,4},{4,5},{5,6},{6,7},{7,0},{8,9},{9,10},{10,1... | collective-permute-start | bytes 55304 | tf_op jit(solution)/shard_map/ppermute | solution.py:18
  129.2 4.1 %collective-permute-start.3 = (f32[18,1,256]{2,1,0:T(1,128)S(1)}, f32[18,1,256]{2,1,0:T(1,128)S(1)}, u32[]{:S(2)}, u32[]{:S(2)}) collective-permute-start(f32[18,1,256]{2,1,0:T(1,128)S(1)} %get-tuple-element.25), channel_id=1, source_target_pairs={{1,0},{2,1},{3,2},{4,3},{5,4},{6,5},{7,6},{0,7},{9,8},{10,9},{11,1... | collective-permute-start | bytes 55304 | tf_op jit(solution)/shard_map/ppermute | solution.py:19
  134.7 94.5 %all-to-all-start.2 = ((bf16[16,24,256]{2,1,0:T(8,128)(2,1)}), bf16[16,24,256]{2,1,0:T(8,128)(2,1)S(1)}, u32[]{:S(2)}, u32[]{:S(2)}) async-start(bf16[16,24,256]{2,1,0:T(8,128)(2,1)} %add_convert_fusion), calls=%async_computation.2 | async-start | bytes 393216 | tf_op jit(solution)/shard_map/all_to_all | solution.py:118
  138.6 91.3 %all-reduce.10.cloned.1.call-start = ((), (), s32[]{:S(2)}) async-start(), calls=%async_computation.5 | async-start | bytes 786432 | tf_op jit(solution)/shard_map/psum | solution.py:144
Sparse Core Ops, SparseCore 0:
  133.1 53.5 all-reduce.7
  189.0 36.7 all-reduce.9
